TPU v7x, 32 devices: a whole 2x2x4 slice. The times are simulated.
32 devices in a mesh: gx: 4 (over y, x), gy: 2 (over core), gz: 4 (over z).
Axes of the slice: x: 2, y: 2, z: 4, core: 2. Of those that a mesh axis runs over, the one named last changes fastest.
Arguments:
- states: float32 [41, 16, 32, 1024], P(None, 'gz', 'gy', 'gx'), may hold values from 0 to 1
- prior_states: float32 [41, 16, 32, 1024], P(None, 'gz', 'gy', 'gx'), may hold values from 0 to 1
- cell_layers: int32 [16, 32, 1024], P('gz', 'gy', 'gx'), may hold values from 0 to 2
- fiber_classes: int32 [16, 32, 1024], P('gz', 'gy', 'gx'), may hold values from 0 to 15
- writer_stripe: int32 [8], replicated, may hold values from 0 to 7, each once
- gate_half: float32 [3, 40], replicated, may hold values from -1 to 1.5
- gate_slope: float32 [3, 40], replicated, may hold values from 1 to 8
- gate_tau: float32 [3, 40], replicated, may hold values from 1 to 40
- gate_conduct: float32 [3, 40], replicated, may hold values from 0.002 to 0.025
- gate_reversal: float32 [3, 40], replicated, may hold values from -1.5 to 1.5
- fiber_conduct: float32 [16, 3], replicated, may hold values from 0.02 to 0.15
Outputs:
- new_states: float32 [41, 16, 32, 1024], P(None, 'gz', 'gy', 'gx')
- stripes: float32 [41, 64, 8, 1024], P(None, ('gy', 'gz'), None, 'gx')
Inputs may be any that keep to these rules, and one draw needn't show every extreme that they name: `writer_stripe`: every one of the 8 stripes has exactly one writer.
All inputs are finite; a program needn't handle non-finite values.
Results may differ from a plain program's by a relative error of at most 0.000062.
Values sent between devices are 32-bit elements; how exact they have to be, the bound alone decides.
A program may use at most 64 MiB of HBM per device.

v0:
```python
import jax
import jax.numpy as jnp
from jax import lax
from jax.sharding import PartitionSpec as P

STEPS = 4


def extended(block, sides, width):
    for axis, dim in sides:
        count = lax.axis_size(axis)
        forward = [(i, i + 1) for i in range(count - 1)]
        backward = [(target, source) for source, target in forward]
        low = lax.ppermute(
            lax.slice_in_dim(block, block.shape[dim] - width, None, axis=dim), axis, forward
        )
        high = lax.ppermute(lax.slice_in_dim(block, 0, width, axis=dim), axis, backward)
        block = jnp.concatenate([low, block, high], axis=dim)
    return block


def pick_layers(cell_layers, params):
    tail_shape = (1,) * cell_layers.ndim
    layer_count = params.shape[0]
    picked = jnp.broadcast_to(
        params[layer_count - 1].reshape((-1,) + tail_shape), (params.shape[1],) + cell_layers.shape
    )
    for which_layer in range(layer_count - 2, -1, -1):
        picked = jnp.where(
            cell_layers[None] == which_layer,
            params[which_layer].reshape((-1,) + tail_shape),
            picked,
        )
    return picked


def edge_masks(device_index, device_count, length, dim):
    position = device_index * length + jnp.arange(length, dtype=jnp.int32)
    extent = length * device_count
    view_shape = [1, 1, 1]
    view_shape[dim] = length
    below_ok = (position > 0).astype(jnp.float32).reshape(view_shape)
    above_ok = (position < extent - 1).astype(jnp.float32).reshape(view_shape)
    return (below_ok, above_ok)


def per_device(
    states,
    prior_states,
    cell_layers,
    fiber_classes,
    writer_stripe,
    gate_half,
    gate_slope,
    gate_tau,
    gate_conduct,
    gate_reversal,
    fiber_conduct,
):
    states_count = prior_states.shape[0]
    writers = lax.axis_size("gy") * lax.axis_size("gz")
    pieces = prior_states.reshape(states_count, writers, -1, prior_states.shape[3])
    outgoing = jnp.take(pieces, writer_stripe, axis=1)
    sectioned = outgoing.reshape(
        states_count, lax.axis_size("gy"), lax.axis_size("gz"), outgoing.shape[2], outgoing.shape[3]
    )
    arrived = lax.all_to_all(
        lax.all_to_all(sectioned, "gy", split_axis=1, concat_axis=1, tiled=True),
        "gz",
        split_axis=2,
        concat_axis=2,
        tiled=True,
    )
    stripes = arrived.reshape(outgoing.shape)
    cells_t, cells_w, cells_d = (states.shape[1], states.shape[2], states.shape[3])
    fibers = fiber_conduct.shape[0]
    onehot = (
        fiber_classes[None] == jnp.arange(fibers, dtype=jnp.int32)[:, None, None, None]
    ).astype(jnp.float32)
    sigma_cells = jnp.dot(
        fiber_conduct.T, onehot.reshape(fibers, -1), precision=lax.Precision.HIGHEST
    )
    sigma_cells = sigma_cells.reshape(3, cells_t, cells_w, cells_d)
    half_cells = pick_layers(cell_layers, gate_half)
    slope_cells = pick_layers(cell_layers, gate_slope)
    tau_cells = pick_layers(cell_layers, gate_tau)
    cond_cells = pick_layers(cell_layers, gate_conduct)
    rev_cells = pick_layers(cell_layers, gate_reversal)
    below_t, above_t = edge_masks(lax.axis_index("gz"), lax.axis_size("gz"), cells_t, 0)
    below_w, above_w = edge_masks(lax.axis_index("gy"), lax.axis_size("gy"), cells_w, 1)
    below_d, above_d = edge_masks(lax.axis_index("gx"), lax.axis_size("gx"), cells_d, 2)
    voltage = states[0]
    gate_states = states[1:]
    for step_index in range(STEPS):
        steady = jax.nn.sigmoid((voltage[None] - half_cells) * slope_cells)
        decay_rate = jnp.exp(-1.0 / (tau_cells * (1.0 + steady)))
        gate_states = steady + (gate_states - steady) * decay_rate
        current = jnp.sum(cond_cells * gate_states * (voltage[None] - rev_cells), axis=0)
        excited = voltage - current
        padded = extended(excited, (("gx", 2), ("gy", 1), ("gz", 0)), 1)
        across = above_t * (padded[2:, 1:-1, 1:-1] - excited) + below_t * (
            padded[:-2, 1:-1, 1:-1] - excited
        )
        widthwise = above_w * (padded[1:-1, 2:, 1:-1] - excited) + below_w * (
            padded[1:-1, :-2, 1:-1] - excited
        )
        depthwise = above_d * (padded[1:-1, 1:-1, 2:] - excited) + below_d * (
            padded[1:-1, 1:-1, :-2] - excited
        )
        voltage = (
            excited
            + sigma_cells[0] * across
            + sigma_cells[1] * widthwise
            + sigma_cells[2] * depthwise
        )
    new_states = jnp.concatenate([voltage[None], gate_states], axis=0)
    return (new_states, stripes)


def solution(mesh):
    in_specs = (
        P(None, "gz", "gy", "gx"),
        P(None, "gz", "gy", "gx"),
        P("gz", "gy", "gx"),
        P("gz", "gy", "gx"),
        P(),
        P(),
        P(),
        P(),
        P(),
        P(),
        P(),
    )
    out_specs = (P(None, "gz", "gy", "gx"), P(None, ("gy", "gz"), None, "gx"))
    return jax.shard_map(
        per_device, mesh=mesh, in_specs=in_specs, out_specs=out_specs, check_vma=False
    )
```

profile of v0, /device:TPU:20, one launch (start us, length us, event | category | flops | bytes accessed | tf_op | source)
XLA Modules:
  0.0 172.9 jit_solution(2424837104830258432)
XLA Ops:
  4.9 6.5 %multiply_reduce_fusion.3 = (f32[4,16,256]{2,1,0:T(8,128)S(1)}, f32[40,4,16,256]{3,2,1,0:T(8,128)}) fusion(f32[40]{0:T(128)S(1)} %get-tuple-element.52, f32[40]{0:T(128)S(1)} %get-tuple-element.53, f32[40]{0:T(128)S(1)} %get-tuple-element.51, f32[4,16,256]{2,1,0:T(8,128)S(1)} %slice_bitcast_fusion, f32[40]{0:T(128)S(1)} %get-tuple-element.49, ...), kind=kLoop, calls=%fused_computation.9 | loop fusion | flops 16367616 | bytes 5409120 | tf_op jit(solution)/shard_map/reduce_sum | solution.py:98
  12.3 3.3 %collective-permute-start.1 = (f32[4,16,1]{2,1,0:T(8,128)S(1)}, f32[4,16,1]{2,1,0:T(8,128)S(1)}, u32[]{:S(2)}, u32[]{:S(2)}) collective-permute-start(f32[4,16,1]{2,1,0:T(8,128)S(1)} %get-tuple-element.35), channel_id=1, source_target_pairs={{8,0},{16,8},{24,16},{9,1},{17,9},{25,17},{10,2},{18,10},{26,18},{... | collective-permute-start | bytes 776 | tf_op jit(solution)/shard_map/ppermute | solution.py:17
  19.2 3.1 %collective-permute-done = f32[4,16,1]{2,1,0:T(8,128)S(1)} collective-permute-done((f32[4,16,1]{2,1,0:T(8,128)S(1)}, f32[4,16,1]{2,1,0:T(8,128)S(1)}, u32[]{:S(2)}, u32[]{:S(2)}) %collective-permute-start) | collective-permute-done | bytes 288 | tf_op jit(solution)/shard_map/ppermute | solution.py:14
  23.7 3.0 %collective-permute-start.2 = (f32[4,1,258]{2,1,0:T(1,128)S(1)}, f32[4,1,258]{2,1,0:T(1,128)S(1)}, u32[]{:S(2)}, u32[]{:S(2)}) collective-permute-start(f32[4,1,258]{2,1,0:T(1,128)S(1)} %get-tuple-element.28), channel_id=1, source_target_pairs={{0,4},{1,5},{2,6},{3,7},{8,12},{9,13},{10,14},{11,15},{16,20},{17,... | collective-permute-start | bytes 12392 | tf_op jit(solution)/shard_map/ppermute | solution.py:14
  30.0 3.5 %collective-permute-start.5 = (f32[1,18,258]{2,1,0:T(8,128)S(1)}, f32[1,18,258]{2,1,0:T(8,128)S(1)}, u32[]{:S(2)}, u32[]{:S(2)}) collective-permute-start(f32[1,18,258]{2,1,0:T(8,128)S(1)} %get-tuple-element.20), channel_id=1, source_target_pairs={{0,1},{1,2},{2,3},{4,5},{5,6},{6,7},{8,9},{9,10},{10,11},{12,13},{... | collective-permute-start | bytes 55736 | tf_op jit(solution)/shard_map/ppermute | solution.py:14
  36.1 6.5 %multiply_reduce_fusion.2 = (f32[4,16,256]{2,1,0:T(8,128)S(1)}, f32[40,4,16,256]{3,2,1,0:T(8,128)}) fusion(f32[4,16,256]{2,1,0:T(8,128)S(1)} %fusion.69, f32[40]{0:T(128)S(1)} %get-tuple-element.52, f32[40]{0:T(128)S(1)} %get-tuple-element.53, f32[40]{0:T(128)S(1)} %get-tuple-element.51, f32[40]{0:T(128)S(1)} %get-tuple-element.49, ...), kind=kLoop, calls=%fused_computation.7 | loop fusion | flops 16367616 | bytes 5409120 | tf_op jit(solution)/shard_map/reduce_sum | solution.py:98
  44.6 3.9 %collective-permute-start.6 = (f32[4,16,1]{2,1,0:T(8,128)S(1)}, f32[4,16,1]{2,1,0:T(8,128)S(1)}, u32[]{:S(2)}, u32[]{:S(2)}) collective-permute-start(f32[4,16,1]{2,1,0:T(8,128)S(1)} %get-tuple-element.34), channel_id=1, source_target_pairs={{0,8},{8,16},{16,24},{1,9},{9,17},{17,25},{2,10},{10,18},{18,26},{... | collective-permute-start | bytes 776 | tf_op jit(solution)/shard_map/ppermute | solution.py:14
  52.7 3.0 %collective-permute-start.8 = (f32[4,1,258]{2,1,0:T(1,128)S(1)}, f32[4,1,258]{2,1,0:T(1,128)S(1)}, u32[]{:S(2)}, u32[]{:S(2)}) collective-permute-start(f32[4,1,258]{2,1,0:T(1,128)S(1)} %get-tuple-element.26), channel_id=1, source_target_pairs={{0,4},{1,5},{2,6},{3,7},{8,12},{9,13},{10,14},{11,15},{16,20},{17,... | collective-permute-start | bytes 12392 | tf_op jit(solution)/shard_map/ppermute | solution.py:14
  62.7 3.5 %collective-permute-start.11 = (f32[1,18,258]{2,1,0:T(8,128)S(1)}, f32[1,18,258]{2,1,0:T(8,128)S(1)}, u32[]{:S(2)}, u32[]{:S(2)}) collective-permute-start(f32[1,18,258]{2,1,0:T(8,128)S(1)} %get-tuple-element.18), channel_id=1, source_target_pairs={{0,1},{1,2},{2,3},{4,5},{5,6},{6,7},{8,9},{9,10},{10,11},{12,13},{... | collective-permute-start | bytes 55736 | tf_op jit(solution)/shard_map/ppermute | solution.py:14
  67.1 5.9 %all_to_all.10 = f32[41,2,4,8,256]{4,3,2,0,1:T(8,128)S(1)} all-to-all(f32[41,2,4,8,256]{4,3,2,0,1:T(8,128)S(1)} %copy.19), channel_id=1, replica_groups=mesh['gx'=4,'gy'=2,'gz'=4] {'gy'}, dimensions={1} | all-to-all | bytes 5373952 | tf_op jit(solution)/shard_map/all_to_all | solution.py:68
  74.9 4.5 %all-to-all-start.1 = ((f32[41,2,4,8,256]{4,3,1,0,2:T(8,128)}), f32[41,2,4,8,256]{4,3,1,0,2:T(8,128)}, u32[]{:S(2)}, u32[]{:S(2)}) async-start(f32[41,2,4,8,256]{4,3,1,0,2:T(8,128)} %copy.20), calls=%async_computation.1 | async-start | bytes 5373952 | tf_op jit(solution)/shard_map/all_to_all | solution.py:67
  79.7 5.6 %multiply_reduce_fusion.1 = (f32[4,16,256]{2,1,0:T(8,128)S(1)}, f32[40,4,16,256]{3,2,1,0:T(8,128)S(1)}) fusion(f32[4,16,256]{2,1,0:T(8,128)S(1)} %fusion.48, f32[40]{0:T(128)S(1)} %get-tuple-element.52, f32[40]{0:T(128)S(1)} %get-tuple-element.53, f32[40]{0:T(128)S(1)} %get-tuple-element.51, f32[40]{0:T(128)S(1)} %get-tuple-element.49, ...), kind=kLoop, calls=%fused_computation.5 | loop fusion | flops 16367616 | bytes 5409120 | tf_op jit(solution)/shard_map/reduce_sum | solution.py:98
  87.3 3.9 %collective-permute-start.12 = (f32[4,16,1]{2,1,0:T(8,128)S(1)}, f32[4,16,1]{2,1,0:T(8,128)S(1)}, u32[]{:S(2)}, u32[]{:S(2)}) collective-permute-start(f32[4,16,1]{2,1,0:T(8,128)S(1)} %get-tuple-element.32), channel_id=1, source_target_pairs={{0,8},{8,16},{16,24},{1,9},{9,17},{17,25},{2,10},{10,18},{18,26},{... | collective-permute-start | bytes 776 | tf_op jit(solution)/shard_map/ppermute | solution.py:14
  91.2 2.8 %collective-permute-done.12 = f32[4,16,1]{2,1,0:T(8,128)S(1)} collective-permute-done((f32[4,16,1]{2,1,0:T(8,128)S(1)}, f32[4,16,1]{2,1,0:T(8,128)S(1)}, u32[]{:S(2)}, u32[]{:S(2)}) %collective-permute-start.12) | collective-permute-done | bytes 288 | tf_op jit(solution)/shard_map/ppermute | solution.py:14
  95.4 3.0 %collective-permute-start.14 = (f32[4,1,258]{2,1,0:T(1,128)S(1)}, f32[4,1,258]{2,1,0:T(1,128)S(1)}, u32[]{:S(2)}, u32[]{:S(2)}) collective-permute-start(f32[4,1,258]{2,1,0:T(1,128)S(1)} %get-tuple-element.24), channel_id=1, source_target_pairs={{0,4},{1,5},{2,6},{3,7},{8,12},{9,13},{10,14},{11,15},{16,20},{17,... | collective-permute-start | bytes 12392 | tf_op jit(solution)/shard_map/ppermute | solution.py:14
  101.7 3.6 %collective-permute-start.17 = (f32[1,18,258]{2,1,0:T(8,128)S(1)}, f32[1,18,258]{2,1,0:T(8,128)S(1)}, u32[]{:S(2)}, u32[]{:S(2)}) collective-permute-start(f32[1,18,258]{2,1,0:T(8,128)S(1)} %get-tuple-element.16), channel_id=1, source_target_pairs={{0,1},{1,2},{2,3},{4,5},{5,6},{6,7},{8,9},{9,10},{10,11},{12,13},{... | collective-permute-start | bytes 55736 | tf_op jit(solution)/shard_map/ppermute | solution.py:14
  105.4 33.2 %collective-permute-done.16 = f32[1,18,258]{2,1,0:T(8,128)S(1)} collective-permute-done((f32[1,18,258]{2,1,0:T(8,128)S(1)}, f32[1,18,258]{2,1,0:T(8,128)S(1)}, u32[]{:S(2)}, u32[]{:S(2)}) %collective-permute-start.16) | collective-permute-done | bytes 18608 | tf_op jit(solution)/shard_map/ppermute | solution.py:17
  139.7 4.2 %multiply_reduce_fusion = (f32[4,16,256]{2,1,0:T(8,128)S(1)}, f32[40,4,16,256]{3,2,1,0:T(8,128)S(1)}) fusion(f32[4,16,256]{2,1,0:T(8,128)S(1)} %fusion.27, f32[40]{0:T(128)S(1)} %get-tuple-element.52, f32[40]{0:T(128)S(1)} %get-tuple-element.53, f32[40]{0:T(128)S(1)} %get-tuple-element.51, f32[40]{0:T(128)S(1)} %get-tuple-element.49, ...), kind=kLoop, calls=%fused_computation.3 | loop fusion | flops 16367616 | bytes 5409120 | tf_op jit(solution)/shard_map/reduce_sum | solution.py:98
  145.9 3.9 %collective-permute-start.18 = (f32[4,16,1]{2,1,0:T(8,128)S(1)}, f32[4,16,1]{2,1,0:T(8,128)S(1)}, u32[]{:S(2)}, u32[]{:S(2)}) collective-permute-start(f32[4,16,1]{2,1,0:T(8,128)S(1)} %get-tuple-element.30), channel_id=1, source_target_pairs={{0,8},{8,16},{16,24},{1,9},{9,17},{17,25},{2,10},{10,18},{18,26},{... | collective-permute-start | bytes 776 | tf_op jit(solution)/shard_map/ppermute | solution.py:14
  149.8 2.8 %collective-permute-done.18 = f32[4,16,1]{2,1,0:T(8,128)S(1)} collective-permute-done((f32[4,16,1]{2,1,0:T(8,128)S(1)}, f32[4,16,1]{2,1,0:T(8,128)S(1)}, u32[]{:S(2)}, u32[]{:S(2)}) %collective-permute-start.18) | collective-permute-done | bytes 288 | tf_op jit(solution)/shard_map/ppermute | solution.py:14
  154.0 3.0 %collective-permute-start.20 = (f32[4,1,258]{2,1,0:T(1,128)S(1)}, f32[4,1,258]{2,1,0:T(1,128)S(1)}, u32[]{:S(2)}, u32[]{:S(2)}) collective-permute-start(f32[4,1,258]{2,1,0:T(1,128)S(1)} %get-tuple-element.22), channel_id=1, source_target_pairs={{0,4},{1,5},{2,6},{3,7},{8,12},{9,13},{10,14},{11,15},{16,20},{17,... | collective-permute-start | bytes 12392 | tf_op jit(solution)/shard_map/ppermute | solution.py:14
  157.9 3.5 %collective-permute-start.22 = (f32[1,18,258]{2,1,0:T(8,128)S(1)}, f32[1,18,258]{2,1,0:T(8,128)S(1)}, u32[]{:S(2)}, u32[]{:S(2)}) collective-permute-start(f32[1,18,258]{2,1,0:T(8,128)S(1)} %get-tuple-element.13), channel_id=1, source_target_pairs={{1,0},{2,1},{3,2},{5,4},{6,5},{7,6},{9,8},{10,9},{11,10},{13,12},{... | collective-permute-start | bytes 55736 | tf_op jit(solution)/shard_map/ppermute | solution.py:17
  163.8 3.5 %collective-permute-done.23 = f32[1,18,258]{2,1,0:T(8,128)S(1)} collective-permute-done((f32[1,18,258]{2,1,0:T(8,128)S(1)}, f32[1,18,258]{2,1,0:T(8,128)S(1)}, u32[]{:S(2)}, u32[]{:S(2)}) %collective-permute-start.23) | collective-permute-done | bytes 18608 | tf_op jit(solution)/shard_map/ppermute | solution.py:14
  169.3 3.7 %copy.21 = f32[41,2,4,8,256]{4,3,2,1,0:T(8,128)} copy(f32[41,2,4,8,256]{4,3,1,0,2:T(8,128)} %all-to-all-done.1) | data formatting | bytes 5373952 | tf_op jit(solution)/shard_map/all_to_all | solution.py:67
  (84 shorter events, 48.2 us)
Async XLA Ops:
  12.3 6.9 %collective-permute-start.1 = (f32[4,16,1]{2,1,0:T(8,128)S(1)}, f32[4,16,1]{2,1,0:T(8,128)S(1)}, u32[]{:S(2)}, u32[]{:S(2)}) collective-permute-start(f32[4,16,1]{2,1,0:T(8,128)S(1)} %get-tuple-element.35), channel_id=1, source_target_pairs={{8,0},{16,8},{24,16},{9,1},{17,9},{25,17},{10,2},{18,10},{26,18},{... | collective-permute-start | bytes 776 | tf_op jit(solution)/shard_map/ppermute | solution.py:17
  15.6 6.7 %collective-permute-start = (f32[4,16,1]{2,1,0:T(8,128)S(1)}, f32[4,16,1]{2,1,0:T(8,128)S(1)}, u32[]{:S(2)}, u32[]{:S(2)}) collective-permute-start(f32[4,16,1]{2,1,0:T(8,128)S(1)} %get-tuple-element.36), channel_id=1, source_target_pairs={{0,8},{8,16},{16,24},{1,9},{9,17},{17,25},{2,10},{10,18},{18,26},{... | collective-permute-start | bytes 776 | tf_op jit(solution)/shard_map/ppermute | solution.py:14
  22.4 4.4 %collective-permute-start.3 = (f32[4,1,258]{2,1,0:T(1,128)S(1)}, f32[4,1,258]{2,1,0:T(1,128)S(1)}, u32[]{:S(2)}, u32[]{:S(2)}) collective-permute-start(f32[4,1,258]{2,1,0:T(1,128)S(1)} %get-tuple-element.27), channel_id=1, source_target_pairs={{4,0},{5,1},{6,2},{7,3},{12,8},{13,9},{14,10},{15,11},{20,16},{21,... | collective-permute-start | bytes 12392 | tf_op jit(solution)/shard_map/ppermute | solution.py:17
  23.7 3.8 %collective-permute-start.2 = (f32[4,1,258]{2,1,0:T(1,128)S(1)}, f32[4,1,258]{2,1,0:T(1,128)S(1)}, u32[]{:S(2)}, u32[]{:S(2)}) collective-permute-start(f32[4,1,258]{2,1,0:T(1,128)S(1)} %get-tuple-element.28), channel_id=1, source_target_pairs={{0,4},{1,5},{2,6},{3,7},{8,12},{9,13},{10,14},{11,15},{16,20},{17,... | collective-permute-start | bytes 12392 | tf_op jit(solution)/shard_map/ppermute | solution.py:14
  27.7 6.0 %collective-permute-start.4 = (f32[1,18,258]{2,1,0:T(8,128)S(1)}, f32[1,18,258]{2,1,0:T(8,128)S(1)}, u32[]{:S(2)}, u32[]{:S(2)}) collective-permute-start(f32[1,18,258]{2,1,0:T(8,128)S(1)} %get-tuple-element.19), channel_id=1, source_target_pairs={{1,0},{2,1},{3,2},{5,4},{6,5},{7,6},{9,8},{10,9},{11,10},{13,12},{... | collective-permute-start | bytes 55736 | tf_op jit(solution)/shard_map/ppermute | solution.py:17
  30.0 5.9 %collective-permute-start.5 = (f32[1,18,258]{2,1,0:T(8,128)S(1)}, f32[1,18,258]{2,1,0:T(8,128)S(1)}, u32[]{:S(2)}, u32[]{:S(2)}) collective-permute-start(f32[1,18,258]{2,1,0:T(8,128)S(1)} %get-tuple-element.20), channel_id=1, source_target_pairs={{0,1},{1,2},{2,3},{4,5},{5,6},{6,7},{8,9},{9,10},{10,11},{12,13},{... | collective-permute-start | bytes 55736 | tf_op jit(solution)/shard_map/ppermute | solution.py:14
  42.7 5.9 %collective-permute-start.7 = (f32[4,16,1]{2,1,0:T(8,128)S(1)}, f32[4,16,1]{2,1,0:T(8,128)S(1)}, u32[]{:S(2)}, u32[]{:S(2)}) collective-permute-start(f32[4,16,1]{2,1,0:T(8,128)S(1)} %get-tuple-element.33), channel_id=1, source_target_pairs={{8,0},{16,8},{24,16},{9,1},{17,9},{25,17},{10,2},{18,10},{26,18},{... | collective-permute-start | bytes 776 | tf_op jit(solution)/shard_map/ppermute | solution.py:17
  44.6 6.7 %collective-permute-start.6 = (f32[4,16,1]{2,1,0:T(8,128)S(1)}, f32[4,16,1]{2,1,0:T(8,128)S(1)}, u32[]{:S(2)}, u32[]{:S(2)}) collective-permute-start(f32[4,16,1]{2,1,0:T(8,128)S(1)} %get-tuple-element.34), channel_id=1, source_target_pairs={{0,8},{8,16},{16,24},{1,9},{9,17},{17,25},{2,10},{10,18},{18,26},{... | collective-permute-start | bytes 776 | tf_op jit(solution)/shard_map/ppermute | solution.py:14
  51.4 8.8 %collective-permute-start.9 = (f32[4,1,258]{2,1,0:T(1,128)S(1)}, f32[4,1,258]{2,1,0:T(1,128)S(1)}, u32[]{:S(2)}, u32[]{:S(2)}) collective-permute-start(f32[4,1,258]{2,1,0:T(1,128)S(1)} %get-tuple-element.25), channel_id=1, source_target_pairs={{4,0},{5,1},{6,2},{7,3},{12,8},{13,9},{14,10},{15,11},{20,16},{21,... | collective-permute-start | bytes 12392 | tf_op jit(solution)/shard_map/ppermute | solution.py:17
  52.7 7.5 %collective-permute-start.8 = (f32[4,1,258]{2,1,0:T(1,128)S(1)}, f32[4,1,258]{2,1,0:T(1,128)S(1)}, u32[]{:S(2)}, u32[]{:S(2)}) collective-permute-start(f32[4,1,258]{2,1,0:T(1,128)S(1)} %get-tuple-element.26), channel_id=1, source_target_pairs={{0,4},{1,5},{2,6},{3,7},{8,12},{9,13},{10,14},{11,15},{16,20},{17,... | collective-permute-start | bytes 12392 | tf_op jit(solution)/shard_map/ppermute | solution.py:14
  60.4 19.1 %collective-permute-start.10 = (f32[1,18,258]{2,1,0:T(8,128)S(1)}, f32[1,18,258]{2,1,0:T(8,128)S(1)}, u32[]{:S(2)}, u32[]{:S(2)}) collective-permute-start(f32[1,18,258]{2,1,0:T(8,128)S(1)} %get-tuple-element.17), channel_id=1, source_target_pairs={{1,0},{2,1},{3,2},{5,4},{6,5},{7,6},{9,8},{10,9},{11,10},{13,12},{... | collective-permute-start | bytes 55736 | tf_op jit(solution)/shard_map/ppermute | solution.py:17
  62.7 16.7 %collective-permute-start.11 = (f32[1,18,258]{2,1,0:T(8,128)S(1)}, f32[1,18,258]{2,1,0:T(8,128)S(1)}, u32[]{:S(2)}, u32[]{:S(2)}) collective-permute-start(f32[1,18,258]{2,1,0:T(8,128)S(1)} %get-tuple-element.18), channel_id=1, source_target_pairs={{0,1},{1,2},{2,3},{4,5},{5,6},{6,7},{8,9},{9,10},{10,11},{12,13},{... | collective-permute-start | bytes 55736 | tf_op jit(solution)/shard_map/ppermute | solution.py:14
  74.9 94.4 %all-to-all-start.1 = ((f32[41,2,4,8,256]{4,3,1,0,2:T(8,128)}), f32[41,2,4,8,256]{4,3,1,0,2:T(8,128)}, u32[]{:S(2)}, u32[]{:S(2)}) async-start(f32[41,2,4,8,256]{4,3,1,0,2:T(8,128)} %copy.20), calls=%async_computation.1 | async-start | bytes 5373952 | tf_op jit(solution)/shard_map/all_to_all | solution.py:67
  85.4 5.8 %collective-permute-start.13 = (f32[4,16,1]{2,1,0:T(8,128)S(1)}, f32[4,16,1]{2,1,0:T(8,128)S(1)}, u32[]{:S(2)}, u32[]{:S(2)}) collective-permute-start(f32[4,16,1]{2,1,0:T(8,128)S(1)} %get-tuple-element.31), channel_id=1, source_target_pairs={{8,0},{16,8},{24,16},{9,1},{17,9},{25,17},{10,2},{18,10},{26,18},{... | collective-permute-start | bytes 776 | tf_op jit(solution)/shard_map/ppermute | solution.py:17
  87.3 6.7 %collective-permute-start.12 = (f32[4,16,1]{2,1,0:T(8,128)S(1)}, f32[4,16,1]{2,1,0:T(8,128)S(1)}, u32[]{:S(2)}, u32[]{:S(2)}) collective-permute-start(f32[4,16,1]{2,1,0:T(8,128)S(1)} %get-tuple-element.32), channel_id=1, source_target_pairs={{0,8},{8,16},{16,24},{1,9},{9,17},{17,25},{2,10},{10,18},{18,26},{... | collective-permute-start | bytes 776 | tf_op jit(solution)/shard_map/ppermute | solution.py:14
  94.1 4.3 %collective-permute-start.15 = (f32[4,1,258]{2,1,0:T(1,128)S(1)}, f32[4,1,258]{2,1,0:T(1,128)S(1)}, u32[]{:S(2)}, u32[]{:S(2)}) collective-permute-start(f32[4,1,258]{2,1,0:T(1,128)S(1)} %get-tuple-element.23), channel_id=1, source_target_pairs={{4,0},{5,1},{6,2},{7,3},{12,8},{13,9},{14,10},{15,11},{20,16},{21,... | collective-permute-start | bytes 12392 | tf_op jit(solution)/shard_map/ppermute | solution.py:17
  95.4 3.8 %collective-permute-start.14 = (f32[4,1,258]{2,1,0:T(1,128)S(1)}, f32[4,1,258]{2,1,0:T(1,128)S(1)}, u32[]{:S(2)}, u32[]{:S(2)}) collective-permute-start(f32[4,1,258]{2,1,0:T(1,128)S(1)} %get-tuple-element.24), channel_id=1, source_target_pairs={{0,4},{1,5},{2,6},{3,7},{8,12},{9,13},{10,14},{11,15},{16,20},{17,... | collective-permute-start | bytes 12392 | tf_op jit(solution)/shard_map/ppermute | solution.py:14
  99.4 39.2 %collective-permute-start.16 = (f32[1,18,258]{2,1,0:T(8,128)S(1)}, f32[1,18,258]{2,1,0:T(8,128)S(1)}, u32[]{:S(2)}, u32[]{:S(2)}) collective-permute-start(f32[1,18,258]{2,1,0:T(8,128)S(1)} %get-tuple-element.15), channel_id=1, source_target_pairs={{1,0},{2,1},{3,2},{5,4},{6,5},{7,6},{9,8},{10,9},{11,10},{13,12},{... | collective-permute-start | bytes 55736 | tf_op jit(solution)/shard_map/ppermute | solution.py:17
  101.7 37.7 %collective-permute-start.17 = (f32[1,18,258]{2,1,0:T(8,128)S(1)}, f32[1,18,258]{2,1,0:T(8,128)S(1)}, u32[]{:S(2)}, u32[]{:S(2)}) collective-permute-start(f32[1,18,258]{2,1,0:T(8,128)S(1)} %get-tuple-element.16), channel_id=1, source_target_pairs={{0,1},{1,2},{2,3},{4,5},{5,6},{6,7},{8,9},{9,10},{10,11},{12,13},{... | collective-permute-start | bytes 55736 | tf_op jit(solution)/shard_map/ppermute | solution.py:14
  143.9 5.8 %collective-permute-start.19 = (f32[4,16,1]{2,1,0:T(8,128)S(1)}, f32[4,16,1]{2,1,0:T(8,128)S(1)}, u32[]{:S(2)}, u32[]{:S(2)}) collective-permute-start(f32[4,16,1]{2,1,0:T(8,128)S(1)} %get-tuple-element.29), channel_id=1, source_target_pairs={{8,0},{16,8},{24,16},{9,1},{17,9},{25,17},{10,2},{18,10},{26,18},{... | collective-permute-start | bytes 776 | tf_op jit(solution)/shard_map/ppermute | solution.py:17
  145.9 6.7 %collective-permute-start.18 = (f32[4,16,1]{2,1,0:T(8,128)S(1)}, f32[4,16,1]{2,1,0:T(8,128)S(1)}, u32[]{:S(2)}, u32[]{:S(2)}) collective-permute-start(f32[4,16,1]{2,1,0:T(8,128)S(1)} %get-tuple-element.30), channel_id=1, source_target_pairs={{0,8},{8,16},{16,24},{1,9},{9,17},{17,25},{2,10},{10,18},{18,26},{... | collective-permute-start | bytes 776 | tf_op jit(solution)/shard_map/ppermute | solution.py:14
  152.7 4.3 %collective-permute-start.21 = (f32[4,1,258]{2,1,0:T(1,128)S(1)}, f32[4,1,258]{2,1,0:T(1,128)S(1)}, u32[]{:S(2)}, u32[]{:S(2)}) collective-permute-start(f32[4,1,258]{2,1,0:T(1,128)S(1)} %get-tuple-element.21), channel_id=1, source_target_pairs={{4,0},{5,1},{6,2},{7,3},{12,8},{13,9},{14,10},{15,11},{20,16},{21,... | collective-permute-start | bytes 12392 | tf_op jit(solution)/shard_map/ppermute | solution.py:17
  157.9 5.9 %collective-permute-start.22 = (f32[1,18,258]{2,1,0:T(8,128)S(1)}, f32[1,18,258]{2,1,0:T(8,128)S(1)}, u32[]{:S(2)}, u32[]{:S(2)}) collective-permute-start(f32[1,18,258]{2,1,0:T(8,128)S(1)} %get-tuple-element.13), channel_id=1, source_target_pairs={{1,0},{2,1},{3,2},{5,4},{6,5},{7,6},{9,8},{10,9},{11,10},{13,12},{... | collective-permute-start | bytes 55736 | tf_op jit(solution)/shard_map/ppermute | solution.py:17
  161.4 5.9 %collective-permute-start.23 = (f32[1,18,258]{2,1,0:T(8,128)S(1)}, f32[1,18,258]{2,1,0:T(8,128)S(1)}, u32[]{:S(2)}, u32[]{:S(2)}) collective-permute-start(f32[1,18,258]{2,1,0:T(8,128)S(1)} %get-tuple-element.14), channel_id=1, source_target_pairs={{0,1},{1,2},{2,3},{4,5},{5,6},{6,7},{8,9},{9,10},{10,11},{12,13},{... | collective-permute-start | bytes 55736 | tf_op jit(solution)/shard_map/ppermute | solution.py:14
  (5 other events, 99.1 us)
where the time goes:
time: 174 us; the launch traced here: 173 us
  starting transfers between devices  68.7 us (39%)
  waiting for transfers between devices  53.7 us (31%)
  other arithmetic  28.4 us (16%)
  local copies, waits for them, and re-layouts  14.6 us (8%)
  blocking collectives  5.89 us (3%)
    ppermute x12, starting transfers between devices, extended(): lax.ppermute(lax.slice_in_dim(block, block.shape[dim] - width, None, axis...  39.3 us
    ppermute x12, waiting for transfers between devices, extended(): lax.ppermute(lax.slice_in_dim(block, 0, width, axis=dim), axis, backward)  33.2 us
    ppermute x12, starting transfers between devices, extended(): lax.ppermute(lax.slice_in_dim(block, 0, width, axis=dim), axis, backward)  24.8 us
    reduce_sum x4, other arithmetic, per_device(): jnp.sum(cond_cells * gate_states * (voltage[None] - rev_cells), axis=0)  22.8 us
    ppermute x12, waiting for transfers between devices, extended(): lax.ppermute(lax.slice_in_dim(block, block.shape[dim] - width, None, axis...  20.5 us
    all_to_all x1, blocking collectives, per_device(): lax.all_to_all(sectioned, 'gy', split_axis=1, concat_axis=1, tiled=True)  5.89 us
    all_to_all x1, starting transfers between devices, per_device(): lax.all_to_all(lax.all_to_all(sectioned, 'gy', split_axis=1, concat_axis=...  4.55 us
    gather x2, local copies, waits for them, and re-layouts, per_device(): outgoing = jnp.take(pieces, writer_stripe, axis=1)  4.38 us
  transfers between devices with their start and end apart: 25, of which 11 were waited for; matrix products, arithmetic and copies ran while one was open for 12% of the time, Pallas kernels for 0%

commit v1 on v0

v1 whole, which is shorter than its diff:
```python
import functools

import jax
import jax.numpy as jnp
from jax import lax
from jax.experimental import pallas as pl
from jax.experimental.pallas import tpu as pltpu
from jax.sharding import PartitionSpec as P

STEPS = 4
MESH = pl.DeviceIdType.MESH
SUB = 8
LANES = 128
LO_T, HI_T, LO_W, HI_W, LO_D, HI_D = range(6)


def kernel(
    sizes,
    states_hbm,
    prior_hbm,
    layers_ref,
    fibers_ref,
    stripe_ref,
    half_ref,
    slope_ref,
    tau_ref,
    cond_ref,
    rev_ref,
    conduct_ref,
    new_hbm,
    arrived_hbm,
    cells,
    prior,
    outgoing,
    excited,
    face_lo_t,
    face_hi_t,
    face_lo_w,
    face_hi_w,
    face_lo_d,
    face_hi_d,
    sigma,
    load_sem,
    store_sem,
    send_sem,
    recv_sem,
    face_send,
    face_recv,
):
    n_gx, n_gy, n_gz = sizes
    writers = n_gy * n_gz
    states_count, cells_t, cells_w, cells_d = cells.shape
    rows = outgoing.shape[2]
    layer_count, gates = half_ref.shape
    gx, gy, gz = lax.axis_index("gx"), lax.axis_index("gy"), lax.axis_index("gz")
    me = gy * n_gz + gz

    load_prior = pltpu.make_async_copy(prior_hbm, prior, load_sem.at[0])
    load_cells = pltpu.make_async_copy(states_hbm, cells, load_sem.at[1])
    load_prior.start()
    load_cells.start()

    barrier = pltpu.get_barrier_semaphore()
    peers = 0
    for shift_y in range(n_gy):
        for shift_z in range(n_gz):
            if shift_y or shift_z:
                target = (gx, lax.rem(gy + shift_y, n_gy), lax.rem(gz + shift_z, n_gz))
                pl.semaphore_signal(barrier, inc=1, device_id=target, device_id_type=MESH)
                peers += 1
    if n_gx > 1:
        for shift in (1, n_gx - 1):
            target = (lax.rem(gx + shift, n_gx), gy, gz)
            pl.semaphore_signal(barrier, inc=1, device_id=target, device_id_type=MESH)
            peers += 1

    load_prior.wait()
    for writer in range(writers):
        outgoing[writer] = prior[:, stripe_ref[writer]]
    if peers:
        pl.semaphore_wait(barrier, peers)

    def piece(target_gy, target_gz):
        target = target_gy * n_gz + target_gz
        return pltpu.make_async_remote_copy(
            src_ref=outgoing.at[target],
            dst_ref=arrived_hbm.at[me],
            send_sem=send_sem.at[target],
            recv_sem=recv_sem.at[me],
            device_id=(gx, target_gy, target_gz),
            device_id_type=MESH,
        )

    batches = [(distance, shift_y) for distance in range(1, n_gz) for shift_y in range(n_gy)]

    def start_batch(batch):
        distance, shift_y = batch
        target_gy = lax.rem(gy + shift_y, n_gy)

        @pl.when(gz + distance < n_gz)
        def _():
            piece(target_gy, gz + distance).start()

        @pl.when(gz >= distance)
        def _():
            piece(target_gy, gz - distance).start()

    per_step = [batches[i : i + 1] for i in range(STEPS)] + [batches[STEPS:]]
    for batch in per_step[0]:
        start_batch(batch)
    for shift_y in range(1, n_gy):
        piece(lax.rem(gy + shift_y, n_gy), gz).start()
    own = pltpu.make_async_copy(outgoing.at[me], arrived_hbm.at[me], load_sem.at[2])
    own.start()

    at_lo = {LO_T: gz == 0, LO_W: gy == 0, LO_D: gx == 0}
    at_hi = {HI_T: gz == n_gz - 1, HI_W: gy == n_gy - 1, HI_D: gx == n_gx - 1}
    landing = {
        LO_T: face_lo_t, HI_T: face_hi_t, LO_W: face_lo_w,
        HI_W: face_hi_w, LO_D: face_lo_d, HI_D: face_hi_d,
    }
    missing = {**at_lo, **at_hi}
    no_target = {
        LO_T: at_hi[HI_T], HI_T: at_lo[LO_T], LO_W: at_hi[HI_W],
        HI_W: at_lo[LO_W], LO_D: at_hi[HI_D], HI_D: at_lo[LO_D],
    }
    for face, ref in landing.items():
        @pl.when(missing[face])
        def _(ref=ref):
            ref[...] = jnp.zeros_like(ref)

    def face_copy(step, face):
        sources = {
            LO_T: (excited.at[step, cells_t - 1], (gx, gy, gz + 1)),
            HI_T: (excited.at[step, 0], (gx, gy, gz - 1)),
            LO_W: (excited.at[step, :, pl.ds(cells_w - SUB, SUB), :], (gx, gy + 1, gz)),
            HI_W: (excited.at[step, :, pl.ds(0, SUB), :], (gx, gy - 1, gz)),
            LO_D: (excited.at[step, :, :, pl.ds(cells_d - LANES, LANES)], (gx + 1, gy, gz)),
            HI_D: (excited.at[step, :, :, pl.ds(0, LANES)], (gx - 1, gy, gz)),
        }
        source, target = sources[face]
        return pltpu.make_async_remote_copy(
            src_ref=source,
            dst_ref=landing[face].at[step],
            send_sem=face_send.at[step, face],
            recv_sem=face_recv.at[step, face],
            device_id=target,
            device_id_type=MESH,
        )

    classes = fibers_ref[...]
    picked = [jnp.full(classes.shape, conduct_ref[0, c], jnp.float32) for c in range(3)]
    for fiber in range(1, conduct_ref.shape[0]):
        hit = classes == fiber
        picked = [jnp.where(hit, conduct_ref[fiber, c], old) for c, old in enumerate(picked)]
    for c in range(3):
        sigma[c] = picked[c]

    load_cells.wait()
    slab = max(1, cells_t // 2)

    def ionic(step):
        for first in range(0, cells_t, slab):
            span = pl.ds(first, slab)
            voltage = cells[0, span]
            layer = layers_ref[span]
            hits = [layer == which for which in range(layer_count - 1)]

            def pick(table, gate):
                value = jnp.full(voltage.shape, table[layer_count - 1, gate], jnp.float32)
                for which in range(layer_count - 2, -1, -1):
                    value = jnp.where(hits[which], table[which, gate], value)
                return value

            def one_gate(gate, current):
                steady = 1.0 / (
                    1.0 + jnp.exp((pick(half_ref, gate) - voltage) * pick(slope_ref, gate))
                )
                decay = jnp.exp(-1.0 / (pick(tau_ref, gate) * (1.0 + steady)))
                value = steady + (cells[gate + 1, span] - steady) * decay
                cells[gate + 1, span] = value
                return current + pick(cond_ref, gate) * value * (voltage - pick(rev_ref, gate))

            current = lax.fori_loop(0, gates, one_gate, jnp.zeros_like(voltage))
            excited[step, span] = voltage - current

    flat = (cells_t * cells_w, cells_d)
    row = lax.broadcasted_iota(jnp.int32, flat, 0) % cells_w
    lane = lax.broadcasted_iota(jnp.int32, flat, 1)

    def factor(flag):
        return 1.0 - flag.astype(jnp.float32)

    def spread(rows_value):
        return jnp.broadcast_to(rows_value, (cells_t, cells_w, cells_d)).reshape(flat)

    def diffuse(step):
        centre3 = excited[step]
        centre = centre3.reshape(flat)
        below = jnp.concatenate([face_lo_t[step][None], centre3[:-1]], axis=0) - centre3
        above = jnp.concatenate([centre3[1:], face_hi_t[step][None]], axis=0) - centre3
        slab_index = lax.broadcasted_iota(jnp.int32, centre3.shape, 0)
        below = jnp.where(slab_index == 0, below * factor(missing[LO_T]), below)
        above = jnp.where(slab_index == cells_t - 1, above * factor(missing[HI_T]), above)
        across = (below + above).reshape(flat)

        low = spread(face_lo_w[step][:, SUB - 1 : SUB, :])
        high = spread(face_hi_w[step][:, 0:1, :])
        below = jnp.where(
            row == 0, (low - centre) * factor(missing[LO_W]), pltpu.roll(centre, 1, 0) - centre
        )
        above = jnp.where(
            row == cells_w - 1,
            (high - centre) * factor(missing[HI_W]),
            pltpu.roll(centre, flat[0] - 1, 0) - centre,
        )
        widthwise = below + above

        low = pltpu.roll(face_lo_d[step].reshape(flat[0], LANES), 1, 1)
        high = pltpu.roll(face_hi_d[step].reshape(flat[0], LANES), LANES - 1, 1)
        low = jnp.concatenate([low] * (cells_d // LANES), axis=1)
        high = jnp.concatenate([high] * (cells_d // LANES), axis=1)
        below = jnp.where(
            lane == 0, (low - centre) * factor(missing[LO_D]), pltpu.roll(centre, 1, 1) - centre
        )
        above = jnp.where(
            lane == cells_d - 1,
            (high - centre) * factor(missing[HI_D]),
            pltpu.roll(centre, cells_d - 1, 1) - centre,
        )
        depthwise = below + above
        voltage = (
            centre
            + sigma[0].reshape(flat) * across
            + sigma[1].reshape(flat) * widthwise
            + sigma[2].reshape(flat) * depthwise
        )
        cells[0] = voltage.reshape(centre3.shape)

    store_gates = pltpu.make_async_copy(
        cells.at[pl.ds(1, gates)], new_hbm.at[pl.ds(1, gates)], store_sem.at[0]
    )
    store_voltage = pltpu.make_async_copy(cells.at[0], new_hbm.at[0], store_sem.at[1])
    for step in range(STEPS):
        ionic(step)
        for face in range(6):
            @pl.when(jnp.logical_not(no_target[face]))
            def _(face=face):
                face_copy(step, face).start()
        for batch in per_step[step + 1]:
            start_batch(batch)
        if step == STEPS - 1:
            store_gates.start()
        for face in range(6):
            @pl.when(jnp.logical_not(missing[face]))
            def _(face=face):
                face_copy(step, face).wait_recv()
        diffuse(step)
    store_voltage.start()

    for step in range(STEPS):
        for face in range(6):
            @pl.when(jnp.logical_not(no_target[face]))
            def _(face=face, step=step):
                face_copy(step, face).wait_send()
    own.wait()
    for shift_y in range(n_gy):
        for shift_z in range(n_gz):
            if shift_y or shift_z:
                source_gy = lax.rem(gy + shift_y, n_gy)
                source_gz = lax.rem(gz + shift_z, n_gz)
                source = source_gy * n_gz + source_gz
                piece(source_gy, source_gz).wait_send()
                pltpu.make_async_remote_copy(
                    src_ref=outgoing.at[source],
                    dst_ref=arrived_hbm.at[source],
                    send_sem=send_sem.at[source],
                    recv_sem=recv_sem.at[source],
                    device_id=(gx, source_gy, source_gz),
                    device_id_type=MESH,
                ).wait_recv()
    store_gates.wait()
    store_voltage.wait()


def per_device(sizes, states, prior_states, cell_layers, fiber_classes, writer_stripe, *tables):
    n_gx, n_gy, n_gz = sizes
    writers = n_gy * n_gz
    count, cells_t, cells_w, cells_d = states.shape
    rows = cells_t * cells_w // writers
    f32 = jnp.float32
    hbm = pl.BlockSpec(memory_space=pl.ANY)
    vmem = pl.BlockSpec(memory_space=pltpu.VMEM)
    smem = pl.BlockSpec(memory_space=pltpu.SMEM)
    new_states, arrived = pl.pallas_call(
        functools.partial(kernel, sizes),
        out_shape=(
            jax.ShapeDtypeStruct(states.shape, f32),
            jax.ShapeDtypeStruct((writers, count, rows, cells_d), f32),
        ),
        in_specs=[hbm, hbm, vmem, vmem] + [smem] * 7,
        out_specs=(hbm, hbm),
        scratch_shapes=[
            pltpu.VMEM(states.shape, f32),
            pltpu.VMEM((count, writers, rows, cells_d), f32),
            pltpu.VMEM((writers, count, rows, cells_d), f32),
            pltpu.VMEM((STEPS, cells_t, cells_w, cells_d), f32),
            pltpu.VMEM((STEPS, cells_w, cells_d), f32),
            pltpu.VMEM((STEPS, cells_w, cells_d), f32),
            pltpu.VMEM((STEPS, cells_t, SUB, cells_d), f32),
            pltpu.VMEM((STEPS, cells_t, SUB, cells_d), f32),
            pltpu.VMEM((STEPS, cells_t, cells_w, LANES), f32),
            pltpu.VMEM((STEPS, cells_t, cells_w, LANES), f32),
            pltpu.VMEM((3, cells_t, cells_w, cells_d), f32),
            pltpu.SemaphoreType.DMA((3,)),
            pltpu.SemaphoreType.DMA((2,)),
            pltpu.SemaphoreType.DMA((writers,)),
            pltpu.SemaphoreType.DMA((writers,)),
            pltpu.SemaphoreType.DMA((STEPS, 6)),
            pltpu.SemaphoreType.DMA((STEPS, 6)),
        ],
        compiler_params=pltpu.CompilerParams(
            collective_id=0, has_side_effects=True, vmem_limit_bytes=48 * 1024 * 1024
        ),
        name="monodomain",
    )(
        states,
        prior_states.reshape(count, writers, rows, cells_d),
        cell_layers,
        fiber_classes,
        writer_stripe,
        *tables,
    )
    return new_states, jnp.swapaxes(arrived, 0, 1)


def solution(mesh):
    cells = P("gz", "gy", "gx")
    whole_states = P(None, "gz", "gy", "gx")
    sizes = (mesh.shape["gx"], mesh.shape["gy"], mesh.shape["gz"])
    return jax.shard_map(
        functools.partial(per_device, sizes),
        mesh=mesh,
        in_specs=(whole_states, whole_states, cells, cells) + (P(),) * 7,
        out_specs=(whole_states, P(None, ("gy", "gz"), None, "gx")),
        check_vma=False,
    )
```

time: 174 us -> 79.4 us (0.46)
  the two profiles are of different devices: /device:TPU:20 before, /device:TPU:0 now
where the time goes in v1:
time: 79.4 us; the launch traced here: 79 us
  Pallas kernels  68.5 us (86%)
  local copies, waits for them, and re-layouts  9.9 us (12%)
    pallas_call x1, Pallas kernels, per_device(): pl.pallas_call(functools.partial(kernel, sizes), out_shape=(jax.ShapeDtyp...  68.5 us
    unnamed x19, local copies, waits for them, and re-layouts  9.9 us

profile of v1, /device:TPU:0, one launch (start us, length us, event | category | flops | bytes accessed | tf_op | source)
XLA Modules:
  0.0 79.0 jit_solution(15287342384167629120)
XLA Ops:
  0.6 0.8 copy.13.conduct_ref
  1.4 0.0 copy-start
  1.4 0.8 %copy-done = s32[4,16,256]{2,1,0:T(8,128)S(1)} copy-done((s32[4,16,256]{2,1,0:T(8,128)S(1)}, s32[4,16,256]{2,1,0:T(8,128)}, u32[]{:S(2)}) %copy-start) | copy-done | bytes 65560
  2.2 0.0 copy-start.1
  2.2 0.8 %copy-done.1 = s32[4,16,256]{2,1,0:T(8,128)S(1)} copy-done((s32[4,16,256]{2,1,0:T(8,128)S(1)}, s32[4,16,256]{2,1,0:T(8,128)}, u32[]{:S(2)}) %copy-start.1) | copy-done | bytes 65560
  3.1 0.0 copy-start.2
  3.1 0.7 copy-done.2
  3.8 0.0 copy-start.3
  3.8 0.7 copy-done.3
  4.4 0.0 copy-start.4
  4.4 0.7 copy-done.4
  5.1 0.0 copy-start.5
  5.1 0.7 copy-done.5
  5.8 0.0 copy-start.6
  5.8 0.7 copy-done.6
  6.5 0.0 copy-start.7
  6.5 0.7 copy-done.7
  7.1 68.5 %monodomain.1 = (f32[41,4,16,256]{3,2,1,0:T(8,128)S(1)}, f32[8,41,8,256]{3,2,1,0:T(8,128)S(1)}) custom-call(f32[41,4,16,256]{3,2,1,0:T(8,128)} %states_hbm.1, f32[41,8,8,256]{3,2,1,0:T(8,128)} %bitcast.3, s32[4,16,256]{2,1,0:T(8,128)S(1)} %copy-done, s32[4,16,256]{2,1,0:T(8,128)S(1)} %copy-done.1, s32[8]{0:T(128)S(1)} %copy-done.7, f32[3,40]{1,0:T(4,128)S(1)} %copy-done.2, ...), custom_call_target="tpu_custom_call" | custom-call | tf_op jit(solution)/shard_map/monodomain/pallas_call | solution.py:295
  75.6 1.9 %copy.14 = f32[41,8,8,256]{3,2,1,0:T(8,128)} copy(f32[41,8,8,256]{3,2,0,1:T(8,128)S(1)} %bitcast.2) | data formatting | bytes 5373952
  77.5 1.5 %copy.16 = f32[41,4,16,256]{3,2,1,0:T(8,128)} copy(f32[41,4,16,256]{3,2,1,0:T(8,128)S(1)} %get-tuple-element.10) | data formatting | bytes 5373952
Async XLA Ops:
  1.4 0.8 %copy-start = (s32[4,16,256]{2,1,0:T(8,128)S(1)}, s32[4,16,256]{2,1,0:T(8,128)}, u32[]{:S(2)}) copy-start(s32[4,16,256]{2,1,0:T(8,128)} %layers_ref.1) | copy-start | bytes 196612
  2.2 0.8 %copy-start.1 = (s32[4,16,256]{2,1,0:T(8,128)S(1)}, s32[4,16,256]{2,1,0:T(8,128)}, u32[]{:S(2)}) copy-start(s32[4,16,256]{2,1,0:T(8,128)} %fibers_ref.1) | copy-start | bytes 196612
  3.1 0.7 copy-start.2
  3.8 0.7 copy-start.3
  4.4 0.7 copy-start.4
  5.1 0.7 copy-start.5
  5.8 0.7 copy-start.6
  6.5 0.7 copy-start.7

commit v2 on v1

--- a/solution.py
+++ b/solution.py
@@ -11,6 +11,9 @@
 MESH = pl.DeviceIdType.MESH
 SUB = 8
 LANES = 128
+OUT_CUTS = 4
+VMEM_BYTES = 67_043_328
+FIRST_BATCHES = 1
 LO_T, HI_T, LO_W, HI_W, LO_D, HI_D = range(6)
 
 
@@ -18,35 +21,11 @@
     sizes,
     states_hbm,
     prior_hbm,
-    layers_ref,
-    fibers_ref,
-    stripe_ref,
-    half_ref,
-    slope_ref,
-    tau_ref,
-    cond_ref,
-    rev_ref,
-    conduct_ref,
-    new_hbm,
-    arrived_hbm,
-    cells,
-    prior,
-    outgoing,
-    excited,
-    face_lo_t,
-    face_hi_t,
-    face_lo_w,
-    face_hi_w,
-    face_lo_d,
-    face_hi_d,
-    sigma,
-    load_sem,
-    store_sem,
-    send_sem,
-    recv_sem,
-    face_send,
-    face_recv,
+    *rest,
 ):
+    small_hbm, (cells, arrived), scratch = rest[:9], rest[9:11], rest[11:]
+    small, (prior, outgoing, excited, face_lo_t, face_hi_t, face_lo_w, face_hi_w, face_lo_d, face_hi_d, sigma, load_sem, small_sem, send_sem, recv_sem, face_send, face_recv) = scratch[:9], scratch[9:]
+    layers_ref, fibers_ref, stripe_ref, half_ref, slope_ref, tau_ref, cond_ref, rev_ref, conduct_ref = small
     n_gx, n_gy, n_gz = sizes
     writers = n_gy * n_gz
     states_count, cells_t, cells_w, cells_d = cells.shape
@@ -56,8 +35,16 @@
     me = gy * n_gz + gz
 
     load_prior = pltpu.make_async_copy(prior_hbm, prior, load_sem.at[0])
+    load_small = [
+        pltpu.make_async_copy(source, target, small_sem.at[i])
+        for i, (source, target) in enumerate(zip(small_hbm, small))
+    ]
     load_cells = pltpu.make_async_copy(states_hbm, cells, load_sem.at[1])
+    load_small[2].start()
     load_prior.start()
+    for i, load in enumerate(load_small):
+        if i != 2:
+            load.start()
     load_cells.start()
 
     barrier = pltpu.get_barrier_semaphore()
@@ -74,6 +61,7 @@
             pl.semaphore_signal(barrier, inc=1, device_id=target, device_id_type=MESH)
             peers += 1
 
+    load_small[2].wait()
     load_prior.wait()
     for writer in range(writers):
         outgoing[writer] = prior[:, stripe_ref[writer]]
@@ -84,7 +72,7 @@
         target = target_gy * n_gz + target_gz
         return pltpu.make_async_remote_copy(
             src_ref=outgoing.at[target],
-            dst_ref=arrived_hbm.at[me],
+            dst_ref=arrived.at[me],
             send_sem=send_sem.at[target],
             recv_sem=recv_sem.at[me],
             device_id=(gx, target_gy, target_gz),
@@ -105,12 +93,14 @@
         def _():
             piece(target_gy, gz - distance).start()
 
-    per_step = [batches[i : i + 1] for i in range(STEPS)] + [batches[STEPS:]]
+    head = FIRST_BATCHES
+    per_step = [batches[:head]] + [batches[head + i : head + i + 1] for i in range(STEPS - 1)]
+    per_step.append(batches[head + STEPS - 1 :])
     for batch in per_step[0]:
         start_batch(batch)
     for shift_y in range(1, n_gy):
         piece(lax.rem(gy + shift_y, n_gy), gz).start()
-    own = pltpu.make_async_copy(outgoing.at[me], arrived_hbm.at[me], load_sem.at[2])
+    own = pltpu.make_async_copy(outgoing.at[me], arrived.at[me], load_sem.at[2])
     own.start()
 
     at_lo = {LO_T: gz == 0, LO_W: gy == 0, LO_D: gx == 0}
@@ -148,11 +138,14 @@
             device_id_type=MESH,
         )
 
+    for i, load in enumerate(load_small):
+        if i != 2:
+            load.wait()
     classes = fibers_ref[...]
-    picked = [jnp.full(classes.shape, conduct_ref[0, c], jnp.float32) for c in range(3)]
-    for fiber in range(1, conduct_ref.shape[0]):
+    picked = [jnp.full(classes.shape, conduct_ref[c, 0], jnp.float32) for c in range(3)]
+    for fiber in range(1, conduct_ref.shape[1]):
         hit = classes == fiber
-        picked = [jnp.where(hit, conduct_ref[fiber, c], old) for c, old in enumerate(picked)]
+        picked = [jnp.where(hit, conduct_ref[c, fiber], old) for c, old in enumerate(picked)]
     for c in range(3):
         sigma[c] = picked[c]
 
@@ -237,10 +230,6 @@
         )
         cells[0] = voltage.reshape(centre3.shape)
 
-    store_gates = pltpu.make_async_copy(
-        cells.at[pl.ds(1, gates)], new_hbm.at[pl.ds(1, gates)], store_sem.at[0]
-    )
-    store_voltage = pltpu.make_async_copy(cells.at[0], new_hbm.at[0], store_sem.at[1])
     for step in range(STEPS):
         ionic(step)
         for face in range(6):
@@ -249,14 +238,11 @@
                 face_copy(step, face).start()
         for batch in per_step[step + 1]:
             start_batch(batch)
-        if step == STEPS - 1:
-            store_gates.start()
         for face in range(6):
             @pl.when(jnp.logical_not(missing[face]))
             def _(face=face):
                 face_copy(step, face).wait_recv()
         diffuse(step)
-    store_voltage.start()
 
     for step in range(STEPS):
         for face in range(6):
@@ -273,14 +259,30 @@
                 piece(source_gy, source_gz).wait_send()
                 pltpu.make_async_remote_copy(
                     src_ref=outgoing.at[source],
-                    dst_ref=arrived_hbm.at[source],
+                    dst_ref=arrived.at[source],
                     send_sem=send_sem.at[source],
                     recv_sem=recv_sem.at[source],
                     device_id=(gx, source_gy, source_gz),
                     device_id_type=MESH,
                 ).wait_recv()
-    store_gates.wait()
-    store_voltage.wait()
+
+
+def write_out(cells, arrived, new_hbm, stripes_hbm, sem):
+    writers, count = arrived.shape[0], cells.shape[0]
+    copies = [
+        pltpu.make_async_copy(arrived.at[q], stripes_hbm.at[:, q], sem.at[q])
+        for q in range(writers)
+    ]
+    bounds = [count * cut // OUT_CUTS for cut in range(OUT_CUTS + 1)]
+    for cut, (first, last) in enumerate(zip(bounds, bounds[1:])):
+        span = pl.ds(first, last - first)
+        copies.append(
+            pltpu.make_async_copy(cells.at[span], new_hbm.at[span], sem.at[writers + cut])
+        )
+    for copy in copies:
+        copy.start()
+    for copy in copies:
+        copy.wait()
 
 
 def per_device(sizes, states, prior_states, cell_layers, fiber_classes, writer_stripe, *tables):
@@ -289,19 +291,22 @@
     count, cells_t, cells_w, cells_d = states.shape
     rows = cells_t * cells_w // writers
     f32 = jnp.float32
-    hbm = pl.BlockSpec(memory_space=pl.ANY)
+    tables = tables[:-1] + (tables[-1].T,)
+    hbm = pl.BlockSpec(memory_space=pltpu.HBM)
     vmem = pl.BlockSpec(memory_space=pltpu.VMEM)
-    smem = pl.BlockSpec(memory_space=pltpu.SMEM)
     new_states, arrived = pl.pallas_call(
         functools.partial(kernel, sizes),
         out_shape=(
-            jax.ShapeDtypeStruct(states.shape, f32),
-            jax.ShapeDtypeStruct((writers, count, rows, cells_d), f32),
+            pltpu.VMEM(states.shape, f32),
+            pltpu.VMEM((writers, count, rows, cells_d), f32),
         ),
-        in_specs=[hbm, hbm, vmem, vmem] + [smem] * 7,
-        out_specs=(hbm, hbm),
+        in_specs=[hbm] * 11,
+        out_specs=(vmem, vmem),
         scratch_shapes=[
-            pltpu.VMEM(states.shape, f32),
+            pltpu.VMEM(cell_layers.shape, jnp.int32),
+            pltpu.VMEM(cell_layers.shape, jnp.int32),
+            pltpu.SMEM(writer_stripe.shape, jnp.int32),
+            *[pltpu.SMEM(table.shape, f32) for table in tables],
             pltpu.VMEM((count, writers, rows, cells_d), f32),
             pltpu.VMEM((writers, count, rows, cells_d), f32),
             pltpu.VMEM((STEPS, cells_t, cells_w, cells_d), f32),
@@ -313,14 +318,14 @@
             pltpu.VMEM((STEPS, cells_t, cells_w, LANES), f32),
             pltpu.VMEM((3, cells_t, cells_w, cells_d), f32),
             pltpu.SemaphoreType.DMA((3,)),
-            pltpu.SemaphoreType.DMA((2,)),
+            pltpu.SemaphoreType.DMA((9,)),
             pltpu.SemaphoreType.DMA((writers,)),
             pltpu.SemaphoreType.DMA((writers,)),
             pltpu.SemaphoreType.DMA((STEPS, 6)),
             pltpu.SemaphoreType.DMA((STEPS, 6)),
         ],
         compiler_params=pltpu.CompilerParams(
-            collective_id=0, has_side_effects=True, vmem_limit_bytes=48 * 1024 * 1024
+            collective_id=0, has_side_effects=True, vmem_limit_bytes=VMEM_BYTES - 0x20000 - 2 * states.size * states.dtype.itemsize
         ),
         name="monodomain",
     )(
@@ -331,7 +336,19 @@
         writer_stripe,
         *tables,
     )
-    return new_states, jnp.swapaxes(arrived, 0, 1)
+    stripes_shape = (count, writers, rows, cells_d)
+    return pl.pallas_call(
+        write_out,
+        out_shape=(
+            jax.ShapeDtypeStruct(states.shape, f32),
+            jax.ShapeDtypeStruct(stripes_shape, f32),
+        ),
+        in_specs=[vmem, vmem],
+        out_specs=(hbm, hbm),
+        scratch_shapes=[pltpu.SemaphoreType.DMA((writers + OUT_CUTS,))],
+        compiler_params=pltpu.CompilerParams(vmem_limit_bytes=1024 * 1024),
+        name="write_out",
+    )(new_states, arrived)
 
 
 def solution(mesh):

time: 79.4 us -> 71 us (0.89)
  local copies, waits for them, and re-layouts: 9.9 us -> 0 us
  Pallas kernels: 68.5 us -> 70.2 us
    unnamed x19 -> x0, local copies, waits for them, and re-layouts: 9.9 us -> none
    pallas_call x1 -> x2, Pallas kernels: 68.5 us -> 70.2 us  [the longest x1 67.7 us: per_device(): pl.pallas_call(functools.partial(kernel, sizes), out_shape=(pltpu.VMEM(st...]
where the time goes in v2:
time: 71 us; the launch traced here: 70.8 us
  Pallas kernels  70.2 us (99%)
    pallas_call x1, Pallas kernels, per_device(): pl.pallas_call(functools.partial(kernel, sizes), out_shape=(pltpu.VMEM(st...  67.7 us
    pallas_call x1, Pallas kernels, per_device(): pl.pallas_call(write_out, out_shape=(jax.ShapeDtypeStruct(states.shape, f...  2.49 us

profile of v2, /device:TPU:0, one launch (start us, length us, event | category | flops | bytes accessed | tf_op | source)
XLA Modules:
  0.0 70.8 jit_solution(16155046947373610712)
XLA Ops:
  0.6 67.7 %monodomain.1 = (f32[41,4,16,256]{3,2,1,0:T(8,128)S(1)}, f32[8,41,8,256]{3,2,1,0:T(8,128)S(1)}) custom-call(f32[41,4,16,256]{3,2,1,0:T(8,128)} %states_hbm.1, f32[41,8,8,256]{3,2,1,0:T(8,128)} %bitcast.2, s32[4,16,256]{2,1,0:T(8,128)} %rest_0_.1, s32[4,16,256]{2,1,0:T(8,128)} %rest_1_.1, s32[8]{0:T(128)} %rest_2_.1, f32[3,40]{1,0:T(4,128)} %rest_3_.1, ...), custom_call_target="tpu_custom_call" | custom-call | tf_op jit(solution)/shard_map/monodomain/pallas_call | solution.py:297
  68.3 2.5 %write_out.1 = (f32[41,4,16,256]{3,2,1,0:T(8,128)}, f32[41,8,8,256]{3,2,1,0:T(8,128)}) custom-call(f32[41,4,16,256]{3,2,1,0:T(8,128)S(1)} %get-tuple-element.4.cells, f32[8,41,8,256]{3,2,1,0:T(8,128)S(1)} %get-tuple-element.5.arrived), custom_call_target="tpu_custom_call" | custom-call | tf_op jit(solution)/shard_map/write_out/pallas_call | solution.py:340

commit v3 on v2

--- a/solution.py
+++ b/solution.py
@@ -11,9 +11,11 @@
 MESH = pl.DeviceIdType.MESH
 SUB = 8
 LANES = 128
-OUT_CUTS = 4
+OUT_CUTS = 8
 VMEM_BYTES = 67_043_328
 FIRST_BATCHES = 1
+UNROLL = 2
+LOG2E = 1.4426950408889634
 LO_T, HI_T, LO_W, HI_W, LO_D, HI_D = range(6)
 
 
@@ -24,7 +26,7 @@
     *rest,
 ):
     small_hbm, (cells, arrived), scratch = rest[:9], rest[9:11], rest[11:]
-    small, (prior, outgoing, excited, face_lo_t, face_hi_t, face_lo_w, face_hi_w, face_lo_d, face_hi_d, sigma, load_sem, small_sem, send_sem, recv_sem, face_send, face_recv) = scratch[:9], scratch[9:]
+    small, (prior, outgoing, excited, face_lo_t, face_hi_t, face_lo_w, face_hi_w, face_lo_d, face_hi_d, sigma, picked_half, picked_slope, picked_rate, picked_cond, picked_rev, load_sem, small_sem, send_sem, recv_sem, face_send, face_recv) = scratch[:9], scratch[9:]
     layers_ref, fibers_ref, stripe_ref, half_ref, slope_ref, tau_ref, cond_ref, rev_ref, conduct_ref = small
     n_gx, n_gy, n_gz = sizes
     writers = n_gy * n_gz
@@ -152,29 +154,52 @@
     load_cells.wait()
     slab = max(1, cells_t // 2)
 
+    def pick_tables(slab_index):
+        layer = layers_ref[slab_index]
+        hits = [layer == which for which in range(layer_count - 1)]
+
+        def pick(values):
+            value = jnp.full(layer.shape, values[-1], jnp.float32)
+            for hit, one in reversed(list(zip(hits, values))):
+                value = jnp.where(hit, one, value)
+            return value
+
+        def one_gate(gate, carry):
+            def of(table):
+                return [table[which, gate] for which in range(layer_count)]
+
+            picked_half[gate, slab_index] = pick(of(half_ref))
+            picked_slope[gate, slab_index] = pick(of(slope_ref)) * LOG2E
+            picked_rate[gate, slab_index] = -LOG2E / pick(of(tau_ref))
+            picked_cond[gate, slab_index] = pick(of(cond_ref))
+            picked_rev[gate, slab_index] = pick(of(rev_ref))
+            return carry
+
+        lax.fori_loop(0, gates, one_gate, 0)
+
+    for slab_index in range(cells_t):
+        pick_tables(slab_index)
+
     def ionic(step):
         for first in range(0, cells_t, slab):
             span = pl.ds(first, slab)
             voltage = cells[0, span]
-            layer = layers_ref[span]
-            hits = [layer == which for which in range(layer_count - 1)]
-
-            def pick(table, gate):
-                value = jnp.full(voltage.shape, table[layer_count - 1, gate], jnp.float32)
-                for which in range(layer_count - 2, -1, -1):
-                    value = jnp.where(hits[which], table[which, gate], value)
-                return value
 
             def one_gate(gate, current):
                 steady = 1.0 / (
-                    1.0 + jnp.exp((pick(half_ref, gate) - voltage) * pick(slope_ref, gate))
+                    1.0
+                    + jnp.exp2((picked_half[gate, span] - voltage) * picked_slope[gate, span])
                 )
-                decay = jnp.exp(-1.0 / (pick(tau_ref, gate) * (1.0 + steady)))
+                decay = jnp.exp2(picked_rate[gate, span] / (1.0 + steady))
                 value = steady + (cells[gate + 1, span] - steady) * decay
                 cells[gate + 1, span] = value
-                return current + pick(cond_ref, gate) * value * (voltage - pick(rev_ref, gate))
-
-            current = lax.fori_loop(0, gates, one_gate, jnp.zeros_like(voltage))
+                return current + picked_cond[gate, span] * value * (
+                    voltage - picked_rev[gate, span]
+                )
+
+            current = lax.fori_loop(
+                0, gates, one_gate, jnp.zeros_like(voltage), unroll=UNROLL
+            )
             excited[step, span] = voltage - current
 
     flat = (cells_t * cells_w, cells_d)
@@ -317,6 +342,7 @@
             pltpu.VMEM((STEPS, cells_t, cells_w, LANES), f32),
             pltpu.VMEM((STEPS, cells_t, cells_w, LANES), f32),
             pltpu.VMEM((3, cells_t, cells_w, cells_d), f32),
+            *[pltpu.VMEM((count - 1, cells_t, cells_w, cells_d), f32)] * 5,
             pltpu.SemaphoreType.DMA((3,)),
             pltpu.SemaphoreType.DMA((9,)),
             pltpu.SemaphoreType.DMA((writers,)),

time: 71 us -> 70.2 us (0.989)
  Pallas kernels: 70.2 us -> 69.4 us
    pallas_call x1, Pallas kernels: 67.7 us -> 66.9 us  [per_device(): pl.pallas_call(functools.partial(kernel, sizes), out_shape=(pltpu.VMEM(st...]
where the time goes in v3:
time: 70.2 us; the launch traced here: 70 us
  Pallas kernels  69.4 us (99%)
    pallas_call x1, Pallas kernels, per_device(): pl.pallas_call(functools.partial(kernel, sizes), out_shape=(pltpu.VMEM(st...  66.9 us
    pallas_call x1, Pallas kernels, per_device(): pl.pallas_call(write_out, out_shape=(jax.ShapeDtypeStruct(states.shape, f...  2.51 us

profile of v3, /device:TPU:0, one launch (start us, length us, event | category | flops | bytes accessed | tf_op | source)
XLA Modules:
  0.0 70.0 jit_solution(5715233403996022222)
XLA Ops:
  0.6 66.9 %monodomain.1 = (f32[41,4,16,256]{3,2,1,0:T(8,128)S(1)}, f32[8,41,8,256]{3,2,1,0:T(8,128)S(1)}) custom-call(f32[41,4,16,256]{3,2,1,0:T(8,128)} %states_hbm.1, f32[41,8,8,256]{3,2,1,0:T(8,128)} %bitcast.2, s32[4,16,256]{2,1,0:T(8,128)} %rest_0_.1, s32[4,16,256]{2,1,0:T(8,128)} %rest_1_.1, s32[8]{0:T(128)} %rest_2_.1, f32[3,40]{1,0:T(4,128)} %rest_3_.1, ...), custom_call_target="tpu_custom_call" | custom-call | tf_op jit(solution)/shard_map/monodomain/pallas_call | solution.py:322
  67.5 2.5 %write_out.1 = (f32[41,4,16,256]{3,2,1,0:T(8,128)}, f32[41,8,8,256]{3,2,1,0:T(8,128)}) custom-call(f32[41,4,16,256]{3,2,1,0:T(8,128)S(1)} %get-tuple-element.4.cells, f32[8,41,8,256]{3,2,1,0:T(8,128)S(1)} %get-tuple-element.5.arrived), custom_call_target="tpu_custom_call" | custom-call | tf_op jit(solution)/shard_map/write_out/pallas_call | solution.py:366
